TPU v7x, 32 devices: a whole 2x2x4 slice. The times are simulated.
32 devices in a mesh: groups: 2 (over x), ctx: 16 (over z, y, core).
Axes of the slice: x: 2, y: 2, z: 4, core: 2. Of those that a mesh axis runs over, the one named last changes fastest.
Arguments:
- queries: bfloat16 [8192, 1024], P(('groups', 'ctx')), parts along dimension 0, may hold values from -7 to 7
- keys: bfloat16 [8192, 128], P(('groups', 'ctx')), parts along dimension 0, may hold values from -7 to 7
- values: bfloat16 [8192, 128], P(('groups', 'ctx')), parts along dimension 0, may hold values from -6 to 6
- span_order: int32 [64], P('groups'), parts along dimension 0, may hold values from 0 to 31, as said below
Outputs:
- attended: bfloat16 [8192, 1024], P(('groups', 'ctx')), parts along dimension 0
There are 2 independent parts, one for each index of `groups`. A program takes and returns all parts, laid end to end along the dimension named above; each array names one. Nothing has to cross between parts.
Inputs may be any that keep to these rules, and one draw needn't show every extreme that they name: A permutation: rows j * 128 to (j + 1) * 128 - 1 hold span span_order[j] of the sequence; for every j, span_order[2 j] + span_order[2 j + 1] = 31.
All inputs are finite; a program needn't handle non-finite values.
Results may differ from a plain program's by a relative error of at most 0.006.
Values may be sent and summed in bfloat16 or wider, within the bound.
A program may use at most 64 MiB of HBM per device.

v0:
```python
import functools
import math

import jax
import jax.numpy as jnp
from jax import lax
from jax.experimental import pallas as pl
from jax.experimental.pallas import tpu as pltpu
from jax.sharding import PartitionSpec as P

UP, DOWN, SIDE, TWIN = 0, 1, 2, 3
NEG = -1e30


def gather_kernel(n, k_ref, v_ref, buf, send_sem, recv_sem):
    lanes = 4
    zs = n // lanes
    me = lax.axis_index("ctx")
    z = me // lanes
    lane = lax.rem(me, lanes)
    y = lane // 2
    c = lax.rem(lane, 2)
    side = z * lanes + (1 - y) * 2 + c
    twin = z * lanes + y * 2 + (1 - c)
    not_top = z < zs - 1
    not_bottom = z > 0
    up = jnp.minimum(me + lanes, n - lanes + lane)
    down = jnp.maximum(me - lanes, lane)
    target = (up, down, side, twin)

    barrier = pltpu.get_barrier_semaphore()

    def greet(who):
        pl.semaphore_signal(
            barrier, inc=1, device_id={"ctx": who}, device_id_type=pl.DeviceIdType.MESH
        )

    greet(side)
    greet(twin)
    pl.when(not_top)(lambda: greet(up))
    pl.when(not_bottom)(lambda: greet(down))
    pl.semaphore_wait(barrier, 2 + not_top.astype(jnp.int32) + not_bottom.astype(jnp.int32))

    def copy(block, kv, route, src=None):
        return pltpu.make_async_remote_copy(
            src_ref=buf.at[block, kv] if src is None else src,
            dst_ref=buf.at[block, kv],
            send_sem=send_sem.at[block, kv, route],
            recv_sem=recv_sem.at[block, kv],
            device_id={"ctx": target[route]},
            device_id_type=pl.DeviceIdType.MESH,
        )

    own = (k_ref, v_ref)
    for kv in range(2):
        pl.when(not_top)(lambda: copy(me, kv, UP, own[kv]).start())
        pl.when(not_bottom)(lambda: copy(me, kv, DOWN, own[kv]).start())
        copy(me, kv, SIDE, own[kv]).start()
        copy(me, kv, TWIN, own[kv]).start()
    buf[me, 0] = k_ref[...]
    buf[me, 1] = v_ref[...]

    def at(zz, yy, cc):
        return zz * lanes + yy * 2 + cc

    def from_line(zz, onward, keep):
        block = at(zz, y, c)
        for kv in range(2):
            copy(block, kv, onward).wait_recv()
            pl.when(keep)(lambda: copy(block, kv, onward).start())
            copy(block, kv, SIDE).start()
            copy(block, kv, TWIN).start()

    def from_side(zz):
        block = at(zz, 1 - y, c)
        for kv in range(2):
            copy(block, kv, TWIN).wait_recv()
            copy(block, kv, TWIN).start()

    def from_twin(zz):
        for yy in (y, 1 - y):
            for kv in range(2):
                copy(at(zz, yy, 1 - c), kv, TWIN).wait_recv()

    def both(s, low, high):
        pl.when(z >= s)(lambda: low(z - s))
        pl.when(z + s < zs)(lambda: high(z + s))

    for s in range(1, zs):
        both(s, lambda zz: from_line(zz, UP, not_top), lambda zz: from_line(zz, DOWN, not_bottom))
        if s == 1:
            from_side(z)
        else:
            both(s - 1, from_side, from_side)
    both(zs - 1, from_side, from_side)
    from_twin(z)
    for s in range(1, zs):
        both(s, from_twin, from_twin)

    for kv in range(2):
        pl.when(not_top)(lambda: copy(me, kv, UP, own[kv]).wait_send())
        pl.when(not_bottom)(lambda: copy(me, kv, DOWN, own[kv]).wait_send())
        copy(me, kv, SIDE, own[kv]).wait_send()
        copy(me, kv, TWIN, own[kv]).wait_send()

    def line_sent(zz, onward, keep):
        for kv in range(2):
            pl.when(keep)(lambda: copy(at(zz, y, c), kv, onward).wait_send())
            copy(at(zz, y, c), kv, SIDE).wait_send()
            copy(at(zz, y, c), kv, TWIN).wait_send()

    def side_sent(zz):
        for kv in range(2):
            copy(at(zz, 1 - y, c), kv, TWIN).wait_send()

    side_sent(z)
    for s in range(1, zs):
        both(s, lambda zz: line_sent(zz, UP, not_top), lambda zz: line_sent(zz, DOWN, not_bottom))
        both(s, side_sent, side_sent)


def attend_kernel(
    n, heads, span, q_ref, kv_ref, order_ref, out_ref, qs, k1, v1, k2, v2, raw1, raw2, w1, w2
):
    head_size = k1.shape[1]
    me = lax.axis_index("ctx")
    first = order_ref[2 * me]
    second = order_ref[2 * me + 1]
    p = jnp.minimum(first, second)
    swapped = second < first
    low_at = swapped.astype(jnp.int32)
    pad_high = lax.rem(p, 2)
    pad_low = 1 - pad_high
    chunks_low = (p + 1 + pad_low) // 2
    halves = (slice(0, span), slice(span, 2 * span))

    def rows_of(slot):
        return pl.ds(pl.multiple_of(slot * span, span), span)

    def put(slot, block, half, is_low):
        k2[rows_of(slot), :] = kv_ref[block, 0, rows_of(half), :]
        value = kv_ref[block, 1, rows_of(half), :]
        zero = jnp.zeros_like(value)
        v2[rows_of(slot), :head_size] = jnp.where(is_low, value, zero)
        v2[rows_of(slot), head_size:] = jnp.where(is_low, zero, value)

    put(1, me, low_at, True)
    put(n, me, low_at, False)
    put(0, me, low_at, True)
    put(n + 1, me, 1 - low_at, False)

    def place(d, carry):
        q = jnp.minimum(order_ref[2 * d], order_ref[2 * d + 1])
        lo = (order_ref[2 * d + 1] < order_ref[2 * d]).astype(jnp.int32)
        is_low = q < p

        @pl.when(q != p)
        def _():
            slot = jnp.where(is_low, q + 1 + pad_low, n + 1 - pad_high - (q - p))
            put(slot, d, jnp.where(is_low, lo, 1 - lo), is_low)

        k1[rows_of(d), :] = kv_ref[d, 0, rows_of(lo), :]
        v1[rows_of(d), :head_size] = kv_ref[d, 1, rows_of(lo), :]
        return carry

    lax.fori_loop(0, n, place, 0)
    v1[:, head_size:] = jnp.ones_like(v1[:, head_size:])
    for h in range(heads):
        cols = slice(h * head_size, (h + 1) * head_size)
        pair = [q_ref[s, cols] for s in halves]
        qs[0, h] = jnp.where(swapped, pair[1], pair[0])
        qs[1, h] = jnp.where(swapped, pair[0], pair[1])

    factor = math.log2(math.e) / math.sqrt(head_size)
    ahead = lax.broadcasted_iota(jnp.int32, (span, span), 1) - lax.broadcasted_iota(
        jnp.int32, (span, span), 0
    )
    kept_first = jnp.concatenate([ahead <= 0, ahead <= span - 2 * span * pad_low], axis=1)
    kept_last = jnp.concatenate([ahead <= span - 2 * span * pad_high, ahead <= 0], axis=1)
    chunks1 = n // 2
    chunks2 = n // 2 + 1
    wide = 2 * span

    def scores(q, keys):
        return (
            lax.dot_general(q, keys, (((1,), (1,)), ((), ())), preferred_element_type=jnp.float32)
            * factor
        )

    def folded(x, op):
        return op(x[:, :span], x[:, span:])

    def one_head(h, b):
        high = jnp.full((span, span), NEG, jnp.float32)
        low = high
        for i in range(chunks1):
            cols = slice(i * wide, (i + 1) * wide)
            score = scores(qs[1, h], k1[cols, :])
            raw1[b, :, cols] = score
            high = jnp.maximum(high, folded(score, jnp.maximum))
        for i in range(chunks2):
            cols = slice(i * wide, (i + 1) * wide)
            is_low = i < chunks_low
            score = scores(qs[1 - is_low.astype(jnp.int32), h], k2[cols, :])
            if i == 0:
                score = jnp.where(kept_first, score, NEG)
            if i == chunks2 - 1:
                score = jnp.where(kept_last, score, NEG)
            raw2[b, :, cols] = score
            most = folded(score, jnp.maximum)
            low = jnp.where(is_low, jnp.maximum(low, most), low)
            high = jnp.where(is_low, high, jnp.maximum(high, most))
        low = jnp.broadcast_to(jnp.max(low, axis=1, keepdims=True), (span, span))
        high = jnp.broadcast_to(jnp.max(high, axis=1, keepdims=True), (span, span))
        for i in range(chunks1):
            cols = slice(i * wide, (i + 1) * wide)
            shift = jnp.concatenate([high, high], axis=1)
            w1[b, :, cols] = jnp.exp2(raw1[b, :, cols] - shift).astype(jnp.bfloat16)
        sum_low = jnp.zeros((span, span), jnp.float32)
        sum_high = sum_low
        for i in range(chunks2):
            cols = slice(i * wide, (i + 1) * wide)
            is_low = i < chunks_low
            shift = jnp.where(is_low, low, high)
            weight = jnp.exp2(raw2[b, :, cols] - jnp.concatenate([shift, shift], axis=1))
            w2[b, :, cols] = weight.astype(jnp.bfloat16)
            add = folded(weight, jnp.add)
            sum_low = jnp.where(is_low, sum_low + add, sum_low)
            sum_high = jnp.where(is_low, sum_high, sum_high + add)
        got1 = jnp.dot(w1[b], v1[...], preferred_element_type=jnp.float32)
        got2 = jnp.dot(w2[b], v2[...], preferred_element_type=jnp.float32)
        sum_low = jnp.sum(sum_low, axis=1, keepdims=True)
        sum_high = jnp.sum(sum_high, axis=1, keepdims=True)
        out_low = got2[:, :head_size] / sum_low
        out_high = (got1[:, :head_size] + got2[:, head_size:]) / (got1[:, head_size:] + sum_high)
        cols = pl.ds(pl.multiple_of(h * head_size, head_size), head_size)
        out_ref[halves[0], cols] = jnp.where(swapped, out_high, out_low).astype(jnp.bfloat16)
        out_ref[halves[1], cols] = jnp.where(swapped, out_low, out_high).astype(jnp.bfloat16)

    together = 2 if chunks1 <= heads else 1

    def some_heads(g, carry):
        for b in range(together):
            one_head(g * together + b, b)
        return carry

    lax.fori_loop(0, heads // together, some_heads, 0)


def body(n, queries, keys, values, span_order):
    local_rows, width = queries.shape
    head_size = keys.shape[1]
    heads = width // head_size
    span = local_rows // 2
    vmem = pl.BlockSpec(memory_space=pltpu.VMEM)
    gathered = pl.pallas_call(
        functools.partial(gather_kernel, n),
        out_shape=jax.ShapeDtypeStruct((n, 2, local_rows, head_size), jnp.bfloat16),
        in_specs=[vmem, vmem],
        out_specs=vmem,
        scratch_shapes=[
            pltpu.SemaphoreType.DMA((n, 2, 4)),
            pltpu.SemaphoreType.DMA((n, 2)),
        ],
        compiler_params=pltpu.CompilerParams(collective_id=0, has_side_effects=True),
        name="gather",
    )(keys, values)
    half_keys = n * span
    more_keys = (n + 2) * span
    return pl.pallas_call(
        functools.partial(attend_kernel, n, heads, span),
        out_shape=jax.ShapeDtypeStruct((local_rows, width), jnp.bfloat16),
        in_specs=[vmem, vmem, pl.BlockSpec(memory_space=pltpu.SMEM)],
        out_specs=vmem,
        scratch_shapes=[
            pltpu.VMEM((2, heads, span, head_size), jnp.bfloat16),
            pltpu.VMEM((half_keys, head_size), jnp.bfloat16),
            pltpu.VMEM((half_keys, 2 * head_size), jnp.bfloat16),
            pltpu.VMEM((more_keys, head_size), jnp.bfloat16),
            pltpu.VMEM((more_keys, 2 * head_size), jnp.bfloat16),
            pltpu.VMEM((2, span, half_keys), jnp.float32),
            pltpu.VMEM((2, span, more_keys), jnp.float32),
            pltpu.VMEM((2, span, half_keys), jnp.bfloat16),
            pltpu.VMEM((2, span, more_keys), jnp.bfloat16),
        ],
        name="attend",
    )(queries, gathered, span_order)


def solution(mesh):
    in_specs = (
        P(("groups", "ctx"), None),
        P(("groups", "ctx"), None),
        P(("groups", "ctx"), None),
        P("groups"),
    )
    out_specs = P(("groups", "ctx"), None)
    return jax.shard_map(
        functools.partial(body, mesh.shape["ctx"]),
        mesh=mesh,
        in_specs=in_specs,
        out_specs=out_specs,
        check_vma=False,
    )
```

profile of v0, /device:TPU:0, one launch (start us, length us, event | category | flops | bytes accessed | tf_op | source)
XLA Modules:
  0.0 36.5 jit_solution(12180387991114226346)
XLA Ops:
  0.0 24.4 %gather.1.kv_ref = bf16[16,2,256,128]{3,2,1,0:T(8,128)(2,1)} custom-call(bf16[256,128]{1,0:T(8,128)(2,1)} %k_ref.1, bf16[256,128]{1,0:T(8,128)(2,1)} %v_ref.1), custom_call_target="tpu_custom_call" | custom-call | tf_op jit(solution)/shard_map/gather/pallas_call | solution.py:256
  24.4 12.1 %attend.1 = bf16[256,1024]{1,0:T(8,128)(2,1)} custom-call(bf16[256,1024]{1,0:T(8,128)(2,1)} %q_ref.1, bf16[16,2,256,128]{3,2,1,0:T(8,128)(2,1)} %gather.1.kv_ref, s32[32]{0:T(128)} %order_ref.1), custom_call_target="tpu_custom_call" | custom-call | tf_op jit(solution)/shard_map/attend/pallas_call | solution.py:270
where the time goes:
time: 36.7 us; the launch traced here: 36.5 us
  Pallas kernels  36.5 us (99%)
    pallas_call x1, Pallas kernels, body(): pl.pallas_call(functools.partial(gather_kernel, n), out_shape=jax.ShapeDt...  24.4 us
    pallas_call x1, Pallas kernels, body(): pl.pallas_call(functools.partial(attend_kernel, n, heads, span), out_shap...  12.1 us

commit v1 on v0

--- a/solution.py
+++ b/solution.py
@@ -10,6 +10,7 @@
 
 UP, DOWN, SIDE, TWIN = 0, 1, 2, 3
 NEG = -1e30
+FUSED_MOST = 32
 
 
 def gather_kernel(n, k_ref, v_ref, buf, send_sem, recv_sem):
@@ -247,7 +248,332 @@
     lax.fori_loop(0, heads // together, some_heads, 0)
 
 
+LOW, HIGH = 0, 1
+EXTRA = 16
+
+
+def fused_kernel(
+    n, heads, span, order_ref, q_hbm, k_hbm, v_hbm, out_ref,
+    buf, q_in, qt, acc, top, raw, part, wide_v, load_sem, send_sem, recv_sem,
+):
+    lanes = 4
+    zs = n // lanes
+    head_size = buf.shape[3]
+    rows = heads * span
+    tile = 2 * span
+    tiles = rows // tile
+    tall = head_size + EXTRA
+    me = lax.axis_index("ctx")
+    z = me // lanes
+    lane = lax.rem(me, lanes)
+    y = lane // 2
+    c = lax.rem(lane, 2)
+    side = z * lanes + (1 - y) * 2 + c
+    twin = z * lanes + y * 2 + (1 - c)
+    not_top = z < zs - 1
+    not_bottom = z > 0
+    up = jnp.minimum(me + lanes, n - lanes + lane)
+    down = jnp.maximum(me - lanes, lane)
+    target = (up, down, side, twin)
+
+    load_k = pltpu.make_async_copy(k_hbm, buf.at[me, 0], load_sem.at[0])
+    load_v = pltpu.make_async_copy(v_hbm, buf.at[me, 1], load_sem.at[1])
+    load_q = pltpu.make_async_copy(q_hbm, q_in, load_sem.at[2])
+    load_k.start()
+    load_v.start()
+    load_q.start()
+
+    barrier = pltpu.get_barrier_semaphore()
+
+    def greet(who):
+        pl.semaphore_signal(
+            barrier, inc=1, device_id={"ctx": who}, device_id_type=pl.DeviceIdType.MESH
+        )
+
+    greet(side)
+    greet(twin)
+    pl.when(not_top)(lambda: greet(up))
+    pl.when(not_bottom)(lambda: greet(down))
+    load_k.wait()
+    load_v.wait()
+    pl.semaphore_wait(barrier, 2 + not_top.astype(jnp.int32) + not_bottom.astype(jnp.int32))
+
+    def copy(block, kv, route):
+        return pltpu.make_async_remote_copy(
+            src_ref=buf.at[block, kv],
+            dst_ref=buf.at[block, kv],
+            send_sem=send_sem.at[block, kv, route],
+            recv_sem=recv_sem.at[block, kv],
+            device_id={"ctx": target[route]},
+            device_id_type=pl.DeviceIdType.MESH,
+        )
+
+    for kv in range(2):
+        pl.when(not_top)(lambda: copy(me, kv, UP).start())
+        pl.when(not_bottom)(lambda: copy(me, kv, DOWN).start())
+        copy(me, kv, SIDE).start()
+        copy(me, kv, TWIN).start()
+
+    def at(zz, yy, cc):
+        return zz * lanes + yy * 2 + cc
+
+    def from_line(zz, onward, keep):
+        block = at(zz, y, c)
+        for kv in range(2):
+            copy(block, kv, onward).wait_recv()
+            pl.when(keep)(lambda: copy(block, kv, onward).start())
+            copy(block, kv, SIDE).start()
+            copy(block, kv, TWIN).start()
+
+    def from_side(zz):
+        block = at(zz, 1 - y, c)
+        for kv in range(2):
+            copy(block, kv, TWIN).wait_recv()
+            copy(block, kv, TWIN).start()
+
+    def from_twin(zz, yy):
+        for kv in range(2):
+            copy(at(zz, yy, 1 - c), kv, TWIN).wait_recv()
+
+    def both(s, low, high):
+        pl.when(z >= s)(lambda: low(z - s))
+        pl.when(z + s < zs)(lambda: high(z + s))
+
+    def lines(s):
+        both(s, lambda zz: from_line(zz, UP, not_top), lambda zz: from_line(zz, DOWN, not_bottom))
+
+    def sides(s):
+        if s == 0:
+            from_side(z)
+        else:
+            both(s, from_side, from_side)
+
+    inner = jnp.minimum(z, zs - 1 - z)
+    outward = jnp.where(z < zs - 1 - z, 1, -1)
+
+    def plane(r):
+        near = z + ((r + 1) // 2) * (1 if r % 2 == 0 else -1)
+        return jnp.where(r <= 2 * inner, near, z + (r - inner) * outward)
+
+    def pair_of(d):
+        first = order_ref[2 * d]
+        second = order_ref[2 * d + 1]
+        return jnp.minimum(first, second), second < first
+
+    p, swapped = pair_of(me)
+    factor = math.log2(math.e) / math.sqrt(head_size)
+    spans = (slice(0, span), slice(span, 2 * span))
+
+    load_q.wait()
+    for h in range(heads):
+        cols = slice(h * head_size, (h + 1) * head_size)
+        dest = slice(h * span, (h + 1) * span)
+        a = q_in[spans[0], cols]
+        b = q_in[spans[1], cols]
+        qt[LOW, :, dest] = jnp.where(swapped, b, a).T
+        qt[HIGH, :, dest] = jnp.where(swapped, a, b).T
+
+    def lane_tile(t):
+        return slice(t * tile, (t + 1) * tile)
+
+    def peak(score):
+        return jnp.max(score.reshape(span // 8, 8, tile), axis=0)
+
+    def spread(m):
+        return jnp.broadcast_to(jnp.max(m, axis=0, keepdims=True), (8, tile))
+
+    def weigh(slot, m):
+        score = raw[slot].reshape(span // 8, 8, tile)
+        return jnp.exp2(score - m[None]).reshape(span, tile).astype(jnp.bfloat16)
+
+    def scores(keys, which, t):
+        return (
+            jnp.dot(keys, qt[which, :, lane_tile(t)], preferred_element_type=jnp.float32) * factor
+        )
+
+    def halves_of(d, kv, flip):
+        a = buf[d, kv, spans[0], :]
+        b = buf[d, kv, spans[1], :]
+        return jnp.where(flip, b, a), jnp.where(flip, a, b)
+
+    ones = jnp.ones((EXTRA, span), jnp.bfloat16)
+    wide_v[head_size:tall, :] = jnp.ones_like(wide_v[head_size:tall, :])
+
+    def own():
+        k_low, k_high = halves_of(me, 0, swapped)
+        v_low, v_high = halves_of(me, 1, swapped)
+        wide_v[:head_size, :span] = v_low.T
+        wide_v[:head_size, span : 2 * span] = v_high.T
+        kept = lax.broadcasted_iota(jnp.int32, (span, tile), 0) <= lax.rem(
+            lax.broadcasted_iota(jnp.int32, (span, tile), 1), span
+        )
+        for t in range(tiles):
+            lt = lane_tile(t)
+            s0 = scores(k_low, HIGH, t)
+            s1 = jnp.where(kept, scores(k_high, HIGH, t), NEG)
+            s2 = jnp.where(kept, scores(k_low, LOW, t), NEG)
+            raw[0], raw[1], raw[2] = s0, s1, s2
+            m_high = spread(jnp.maximum(peak(s0), peak(s1)))
+            m_low = spread(peak(s2))
+            top[HIGH, :, lt] = m_high
+            top[LOW, :, lt] = m_low
+            part[0, :span, :] = weigh(0, m_high)
+            part[0, span : 2 * span, :] = weigh(1, m_high)
+            part[1, :span, :] = weigh(2, m_low)
+            acc[HIGH, :, lt] = jnp.dot(
+                wide_v[:tall, : 2 * span], part[0, : 2 * span, :], preferred_element_type=jnp.float32
+            )
+            acc[LOW, :, lt] = jnp.dot(
+                wide_v[:tall, :span], part[1, :span, :], preferred_element_type=jnp.float32
+            )
+
+    def group(blocks, between=()):
+        g = len(blocks)
+        depth = g * span
+        info = []
+        for j, d in enumerate(blocks):
+            q, flip = pair_of(d)
+            is_low = q < p
+            k_low, k_high = halves_of(d, 0, flip)
+            v_low, v_high = halves_of(d, 1, flip)
+            at_j = slice(j * span, (j + 1) * span)
+            wide_v[:head_size, at_j] = v_low.T
+            v_x = jnp.where(is_low, v_low, v_high).T
+            nil = jnp.zeros_like(v_x)
+            wide_v[tall : tall + head_size, at_j] = jnp.where(is_low, v_x, nil)
+            wide_v[tall + head_size : 2 * tall, at_j] = jnp.where(is_low, ones, jnp.zeros_like(ones))
+            wide_v[2 * tall : 2 * tall + head_size, at_j] = jnp.where(is_low, nil, v_x)
+            wide_v[2 * tall + head_size :, at_j] = jnp.where(is_low, jnp.zeros_like(ones), ones)
+            info.append((is_low, k_low, jnp.where(is_low, k_low, k_high)))
+        for t in range(tiles):
+            lt = lane_tile(t)
+            old_high = top[HIGH, :, lt]
+            old_low = top[LOW, :, lt]
+            high, low = old_high, old_low
+            base = (t % 2) * 8
+            for j, (is_low, k_low, k_x) in enumerate(info):
+                s = scores(k_low, HIGH, t)
+                raw[base + 2 * j] = s
+                high = jnp.maximum(high, peak(s))
+                s = scores(k_x, 1 - is_low.astype(jnp.int32), t)
+                raw[base + 2 * j + 1] = s
+                m = peak(s)
+                low = jnp.where(is_low, jnp.maximum(low, m), low)
+                high = jnp.where(is_low, high, jnp.maximum(high, m))
+            high = spread(high)
+            low = spread(low)
+            top[HIGH, :, lt] = high
+            top[LOW, :, lt] = low
+            pb = (t % 2) * 2
+            for j, (is_low, _, _) in enumerate(info):
+                at_j = slice(j * span, (j + 1) * span)
+                part[pb, at_j, :] = weigh(base + 2 * j, high)
+                part[pb + 1, at_j, :] = weigh(base + 2 * j + 1, jnp.where(is_low, low, high))
+            more = jnp.dot(
+                wide_v[:tall, :depth], part[pb, :depth, :], preferred_element_type=jnp.float32
+            )
+            mixed = jnp.dot(
+                wide_v[tall:, :depth], part[pb + 1, :depth, :], preferred_element_type=jnp.float32
+            )
+
+            def scaled(which, old, new):
+                return (
+                    acc[which, :, lt].reshape(tall // 8, 8, tile) * jnp.exp2(old - new)[None]
+                ).reshape(tall, tile)
+
+            acc[HIGH, :, lt] = scaled(HIGH, old_high, high) + (more + mixed[tall:])
+            acc[LOW, :, lt] = scaled(LOW, old_low, low) + mixed[:tall]
+            if t < len(between):
+                between[t]()
+
+    own()
+    lines(1)
+    sides(0)
+    from_twin(z, y)
+    from_twin(z, 1 - y)
+    group([twin, side, at(z, 1 - y, 1 - c)])
+    for r in range(1, zs):
+        if r + 1 < zs:
+            lines(r + 1)
+        sides(r)
+        zz = plane(r)
+        if r + 1 == zs:
+            from_twin(zz, y)
+            group([at(zz, y, c), at(zz, y, 1 - c)])
+            from_twin(zz, 1 - y)
+            group([at(zz, 1 - y, c), at(zz, 1 - y, 1 - c)])
+        else:
+            from_twin(zz, y)
+            from_twin(zz, 1 - y)
+            group([at(zz, y, c), at(zz, y, 1 - c), at(zz, 1 - y, c), at(zz, 1 - y, 1 - c)])
+
+    for h in range(heads):
+        cols = slice(h * head_size, (h + 1) * head_size)
+        src = slice(h * span, (h + 1) * span)
+        outs = []
+        for which in (LOW, HIGH):
+            total = acc[which, head_size : head_size + 8, src]
+            share = acc[which, :head_size, src].reshape(head_size // 8, 8, span) / total[None]
+            outs.append(share.reshape(head_size, span).astype(jnp.bfloat16).T)
+        out_ref[spans[0], cols] = jnp.where(swapped, outs[HIGH], outs[LOW])
+        out_ref[spans[1], cols] = jnp.where(swapped, outs[LOW], outs[HIGH])
+
+    for kv in range(2):
+        pl.when(not_top)(lambda: copy(me, kv, UP).wait_send())
+        pl.when(not_bottom)(lambda: copy(me, kv, DOWN).wait_send())
+        copy(me, kv, SIDE).wait_send()
+        copy(me, kv, TWIN).wait_send()
+
+    def line_sent(zz, onward, keep):
+        for kv in range(2):
+            pl.when(keep)(lambda: copy(at(zz, y, c), kv, onward).wait_send())
+            copy(at(zz, y, c), kv, SIDE).wait_send()
+            copy(at(zz, y, c), kv, TWIN).wait_send()
+
+    def side_sent(zz):
+        for kv in range(2):
+            copy(at(zz, 1 - y, c), kv, TWIN).wait_send()
+
+    side_sent(z)
+    for s in range(1, zs):
+        both(s, lambda zz: line_sent(zz, UP, not_top), lambda zz: line_sent(zz, DOWN, not_bottom))
+        both(s, side_sent, side_sent)
+
+
+def fused(n, queries, keys, values, span_order):
+    local_rows, width = queries.shape
+    head_size = keys.shape[1]
+    heads = width // head_size
+    span = local_rows // 2
+    rows = heads * span
+    anywhere = pl.BlockSpec(memory_space=pl.ANY)
+    tall = head_size + EXTRA
+    return pl.pallas_call(
+        functools.partial(fused_kernel, n, heads, span),
+        out_shape=jax.ShapeDtypeStruct((local_rows, width), jnp.bfloat16),
+        in_specs=[pl.BlockSpec(memory_space=pltpu.SMEM), anywhere, anywhere, anywhere],
+        out_specs=pl.BlockSpec(memory_space=pltpu.VMEM),
+        scratch_shapes=[
+            pltpu.VMEM((n, 2, local_rows, head_size), jnp.bfloat16),
+            pltpu.VMEM((local_rows, width), jnp.bfloat16),
+            pltpu.VMEM((2, head_size, rows), jnp.bfloat16),
+            pltpu.VMEM((2, tall, rows), jnp.float32),
+            pltpu.VMEM((2, 8, rows), jnp.float32),
+            pltpu.VMEM((16, span, 2 * span), jnp.float32),
+            pltpu.VMEM((4, 4 * span, 2 * span), jnp.bfloat16),
+            pltpu.VMEM((3 * tall, 4 * span), jnp.bfloat16),
+            pltpu.SemaphoreType.DMA((3,)),
+            pltpu.SemaphoreType.DMA((n, 2, 4)),
+            pltpu.SemaphoreType.DMA((n, 2)),
+        ],
+        compiler_params=pltpu.CompilerParams(collective_id=0, has_side_effects=True),
+        name="fused",
+    )(span_order, queries, keys, values)
+
+
 def body(n, queries, keys, values, span_order):
+    if n <= FUSED_MOST:
+        return fused(n, queries, keys, values, span_order)
     local_rows, width = queries.shape
     head_size = keys.shape[1]
     heads = width // head_size

time: 36.7 us -> 29.3 us (0.80)
  Pallas kernels: 36.5 us -> 27.3 us
  local copies, waits for them, and re-layouts: 0 us -> 1.87 us
    pallas_call x2 -> x1, Pallas kernels: 36.5 us -> 27.3 us  [fused(): pl.pallas_call(functools.partial(fused_kernel, n, heads, span), out_shape...]
    unnamed x0 -> x1, local copies, waits for them, and re-layouts: none -> 1.87 us
where the time goes in v1:
time: 29.3 us; the launch traced here: 29.1 us
  Pallas kernels  27.3 us (93%)
  local copies, waits for them, and re-layouts  1.87 us (6%)
    pallas_call x1, Pallas kernels, fused(): pl.pallas_call(functools.partial(fused_kernel, n, heads, span), out_shape...  27.3 us
    unnamed x1, local copies, waits for them, and re-layouts  1.87 us

profile of v1, /device:TPU:0, one launch (start us, length us, event | category | flops | bytes accessed | tf_op | source)
XLA Modules:
  0.0 29.1 jit_solution(3739124708004496975)
XLA Ops:
  0.0 27.3 %fused.1 = bf16[256,1024]{1,0:T(8,128)(2,1)} custom-call(s32[32]{0:T(128)} %order_ref.1, bf16[256,1024]{1,0:T(8,128)(2,1)} %q_hbm.1, bf16[256,128]{1,0:T(8,128)(2,1)} %k_hbm.1, bf16[256,128]{1,0:T(8,128)(2,1)} %v_hbm.1), custom_call_target="tpu_custom_call" | custom-call | tf_op jit(solution)/shard_map/fused/pallas_call | solution.py:551
  27.3 1.9 %copy.6 = bf16[256,1024]{1,0:T(8,128)(2,1)} copy(bf16[256,1024]{1,0:T(8,128)(2,1)} %fused.1) | data formatting | bytes 1048576

commit v2 on v1

--- a/solution.py
+++ b/solution.py
@@ -11,6 +11,9 @@
 UP, DOWN, SIDE, TWIN = 0, 1, 2, 3
 NEG = -1e30
 FUSED_MOST = 32
+PIECES = 2
+RELIEF = True
+GRANT = 24 << 20
 
 
 def gather_kernel(n, k_ref, v_ref, buf, send_sem, recv_sem):
@@ -253,8 +256,8 @@
 
 
 def fused_kernel(
-    n, heads, span, order_ref, q_hbm, k_hbm, v_hbm, out_ref,
-    buf, q_in, qt, acc, top, raw, part, wide_v, load_sem, send_sem, recv_sem,
+    n, heads, span, order_hbm, q_hbm, k_hbm, v_hbm, acc,
+    order_ref, buf, q_in, qt, top, raw, part, wide_v, load_sem, send_sem, line_sem, side_sem, twin_sem,
 ):
     lanes = 4
     zs = n // lanes
@@ -279,8 +282,10 @@
     load_k = pltpu.make_async_copy(k_hbm, buf.at[me, 0], load_sem.at[0])
     load_v = pltpu.make_async_copy(v_hbm, buf.at[me, 1], load_sem.at[1])
     load_q = pltpu.make_async_copy(q_hbm, q_in, load_sem.at[2])
+    load_order = pltpu.make_async_copy(order_hbm, order_ref, load_sem.at[3])
     load_k.start()
     load_v.start()
+    load_order.start()
     load_q.start()
 
     barrier = pltpu.get_barrier_semaphore()
@@ -298,55 +303,127 @@
     load_v.wait()
     pl.semaphore_wait(barrier, 2 + not_top.astype(jnp.int32) + not_bottom.astype(jnp.int32))
 
-    def copy(block, kv, route):
+    piece = span * 2 // PIECES
+
+    def copy(zz, yy, kv, part_of, route):
+        block = at(zz, yy, c)
+        where = buf.at[block, kv, pl.ds(part_of * piece, piece)]
+        other = yy is not y
+        if route == SIDE:
+            landed = side_sem.at[zz, kv, part_of]
+        elif route == TWIN:
+            landed = twin_sem.at[zz, int(other)]
+        elif other:
+            landed = side_sem.at[zz, kv, part_of]
+        else:
+            landed = line_sem.at[zz, kv, part_of]
         return pltpu.make_async_remote_copy(
-            src_ref=buf.at[block, kv],
-            dst_ref=buf.at[block, kv],
-            send_sem=send_sem.at[block, kv, route],
-            recv_sem=recv_sem.at[block, kv],
+            src_ref=where,
+            dst_ref=where,
+            send_sem=send_sem.at[route],
+            recv_sem=landed,
             device_id={"ctx": target[route]},
             device_id_type=pl.DeviceIdType.MESH,
         )
 
-    for kv in range(2):
-        pl.when(not_top)(lambda: copy(me, kv, UP).start())
-        pl.when(not_bottom)(lambda: copy(me, kv, DOWN).start())
-        copy(me, kv, SIDE).start()
-        copy(me, kv, TWIN).start()
-
     def at(zz, yy, cc):
         return zz * lanes + yy * 2 + cc
 
-    def from_line(zz, onward, keep):
-        block = at(zz, y, c)
+    far_y = 1 - y
+    at_bottom = z == 0
+    at_top = z == zs - 1
+
+    def early(zz, kv):
+        if kv == 0 or zs <= 2 or not RELIEF:
+            return jnp.bool_(False)
+        return jnp.logical_or(zz == 0, zz == zs - 1)
+
+    def sends_own(act):
         for kv in range(2):
-            copy(block, kv, onward).wait_recv()
-            pl.when(keep)(lambda: copy(block, kv, onward).start())
-            copy(block, kv, SIDE).start()
-            copy(block, kv, TWIN).start()
-
-    def from_side(zz):
-        block = at(zz, 1 - y, c)
-        for kv in range(2):
-            copy(block, kv, TWIN).wait_recv()
-            copy(block, kv, TWIN).start()
-
-    def from_twin(zz, yy):
-        for kv in range(2):
-            copy(at(zz, yy, 1 - c), kv, TWIN).wait_recv()
+            for i in range(PIECES):
+                pl.when(not_top)(lambda: act(copy(z, y, kv, i, UP)))
+                pl.when(not_bottom)(lambda: act(copy(z, y, kv, i, DOWN)))
+                act(copy(z, y, kv, i, SIDE))
+                act(copy(z, y, kv, i, TWIN))
+
+    def sends_line(zz, kv, i, onward, act):
+        pl.when(not_top if onward == UP else not_bottom)(lambda: act(copy(zz, y, kv, i, onward)))
+        pl.when(jnp.logical_not(early(zz, kv)))(lambda: act(copy(zz, y, kv, i, SIDE)))
+        act(copy(zz, y, kv, i, TWIN))
+
+    def sends_side(zz, kv, i, onward, act):
+        more = not_top if onward == UP else not_bottom
+        if kv == 1 and zs > 2 and RELIEF:
+            pl.when(jnp.logical_and(early(zz, kv), more))(lambda: act(copy(zz, far_y, kv, i, onward)))
+        act(copy(zz, far_y, kv, i, TWIN))
+
+    def sends_near(kv, i, act):
+        if kv == 1 and zs > 2 and RELIEF:
+            pl.when(at_bottom)(lambda: act(copy(z, far_y, kv, i, UP)))
+            pl.when(at_top)(lambda: act(copy(z, far_y, kv, i, DOWN)))
+        act(copy(z, far_y, kv, i, TWIN))
+
+    def begin(one):
+        one.start()
+
+    def arrived(zz, yy, kv, i):
+        where = buf.at[at(zz, yy, c), kv, pl.ds(i * piece, piece)]
+        sem = (line_sem if yy is y else side_sem).at[zz, kv, i]
+        pltpu.make_async_copy(where, where, sem).wait()
 
     def both(s, low, high):
         pl.when(z >= s)(lambda: low(z - s))
         pl.when(z + s < zs)(lambda: high(z + s))
 
-    def lines(s):
-        both(s, lambda zz: from_line(zz, UP, not_top), lambda zz: from_line(zz, DOWN, not_bottom))
-
-    def sides(s):
-        if s == 0:
-            from_side(z)
+    def line_event(s, kv, i):
+        def arrive(zz, onward):
+            arrived(zz, y, kv, i)
+            sends_line(zz, kv, i, onward, begin)
+
+        both(s, lambda zz: arrive(zz, UP), lambda zz: arrive(zz, DOWN))
+
+    def side_event(s, kv, i):
+        def arrive(zz, onward):
+            arrived(zz, far_y, kv, i)
+            sends_side(zz, kv, i, onward, begin)
+
+        if s:
+            both(s, lambda zz: arrive(zz, UP), lambda zz: arrive(zz, DOWN))
         else:
-            both(s, from_side, from_side)
+            arrived(z, far_y, kv, i)
+            sends_near(kv, i, begin)
+
+    def events(kind, s):
+        return [functools.partial(kind, s, kv, i) for kv in range(2) for i in range(PIECES)]
+
+    def from_twin(zz, yy):
+        where = buf.at[at(zz, yy, 1 - c)]
+        pltpu.make_async_copy(where, where, twin_sem.at[zz, int(yy is not y)]).wait()
+
+    def all_sent():
+        def taken(arrays, route):
+            blocks = arrays // 2
+            where = buf.at[pl.ds(0, blocks)] if blocks else buf.at[0, 0]
+            pltpu.make_async_copy(where, where, send_sem.at[route]).wait()
+
+        taken(4 * zs, TWIN)
+        if not RELIEF or zs <= 2:
+            taken(2 * zs, SIDE)
+            for zz in range(zs):
+                pl.when(jnp.logical_and(not_top, zz <= z))(lambda: taken(2, UP))
+                pl.when(jnp.logical_and(not_bottom, zz >= z))(lambda: taken(2, DOWN))
+        else:
+            taken(2, SIDE)
+            for zz in range(zs):
+                pl.when(zz != z)(lambda: taken(1, SIDE))
+                if 0 < zz < zs - 1:
+                    pl.when(zz != z)(lambda: taken(1, SIDE))
+                pl.when(jnp.logical_and(not_top, zz <= z))(lambda: taken(2, UP))
+                pl.when(jnp.logical_and(not_bottom, zz >= z))(lambda: taken(2, DOWN))
+            pl.when(not_top)(lambda: taken(1, UP))
+            pl.when(not_bottom)(lambda: taken(1, DOWN))
+
+    sends_own(begin)
 
     inner = jnp.minimum(z, zs - 1 - z)
     outward = jnp.where(z < zs - 1 - z, 1, -1)
@@ -360,6 +437,7 @@
         second = order_ref[2 * d + 1]
         return jnp.minimum(first, second), second < first
 
+    load_order.wait()
     p, swapped = pair_of(me)
     factor = math.log2(math.e) / math.sqrt(head_size)
     spans = (slice(0, span), slice(span, 2 * span))
@@ -487,26 +565,41 @@
                 between[t]()
 
     own()
-    lines(1)
-    sides(0)
+    def run(todo):
+        for one in todo:
+            one()
+
+    def mixed(a, b):
+        return [one for pair in zip(a, b) for one in pair]
+
+    run(mixed(events(line_event, 1), events(side_event, 0)))
     from_twin(z, y)
-    from_twin(z, 1 - y)
+    from_twin(z, far_y)
     group([twin, side, at(z, 1 - y, 1 - c)])
     for r in range(1, zs):
         if r + 1 < zs:
-            lines(r + 1)
-        sides(r)
+            run(mixed(events(line_event, r + 1), events(side_event, r)))
+        else:
+            run(events(side_event, r))
         zz = plane(r)
         if r + 1 == zs:
             from_twin(zz, y)
             group([at(zz, y, c), at(zz, y, 1 - c)])
-            from_twin(zz, 1 - y)
+            from_twin(zz, far_y)
             group([at(zz, 1 - y, c), at(zz, 1 - y, 1 - c)])
         else:
             from_twin(zz, y)
-            from_twin(zz, 1 - y)
+            from_twin(zz, far_y)
             group([at(zz, y, c), at(zz, y, 1 - c), at(zz, 1 - y, c), at(zz, 1 - y, 1 - c)])
 
+    all_sent()
+
+
+def share_kernel(heads, span, order_ref, acc, out_ref):
+    head_size = out_ref.shape[1] // heads
+    spans = (slice(0, span), slice(span, 2 * span))
+    me = lax.axis_index("ctx")
+    swapped = order_ref[2 * me + 1] < order_ref[2 * me]
     for h in range(heads):
         cols = slice(h * head_size, (h + 1) * head_size)
         src = slice(h * span, (h + 1) * span)
@@ -518,27 +611,6 @@
         out_ref[spans[0], cols] = jnp.where(swapped, outs[HIGH], outs[LOW])
         out_ref[spans[1], cols] = jnp.where(swapped, outs[LOW], outs[HIGH])
 
-    for kv in range(2):
-        pl.when(not_top)(lambda: copy(me, kv, UP).wait_send())
-        pl.when(not_bottom)(lambda: copy(me, kv, DOWN).wait_send())
-        copy(me, kv, SIDE).wait_send()
-        copy(me, kv, TWIN).wait_send()
-
-    def line_sent(zz, onward, keep):
-        for kv in range(2):
-            pl.when(keep)(lambda: copy(at(zz, y, c), kv, onward).wait_send())
-            copy(at(zz, y, c), kv, SIDE).wait_send()
-            copy(at(zz, y, c), kv, TWIN).wait_send()
-
-    def side_sent(zz):
-        for kv in range(2):
-            copy(at(zz, 1 - y, c), kv, TWIN).wait_send()
-
-    side_sent(z)
-    for s in range(1, zs):
-        both(s, lambda zz: line_sent(zz, UP, not_top), lambda zz: line_sent(zz, DOWN, not_bottom))
-        both(s, side_sent, side_sent)
-
 
 def fused(n, queries, keys, values, span_order):
     local_rows, width = queries.shape
@@ -546,29 +618,42 @@
     heads = width // head_size
     span = local_rows // 2
     rows = heads * span
-    anywhere = pl.BlockSpec(memory_space=pl.ANY)
+    anywhere = pl.BlockSpec(memory_space=pltpu.HBM)
     tall = head_size + EXTRA
-    return pl.pallas_call(
+    vmem = pl.BlockSpec(memory_space=pltpu.VMEM)
+    acc = pl.pallas_call(
         functools.partial(fused_kernel, n, heads, span),
-        out_shape=jax.ShapeDtypeStruct((local_rows, width), jnp.bfloat16),
-        in_specs=[pl.BlockSpec(memory_space=pltpu.SMEM), anywhere, anywhere, anywhere],
-        out_specs=pl.BlockSpec(memory_space=pltpu.VMEM),
+        out_shape=jax.ShapeDtypeStruct((2, tall, rows), jnp.float32),
+        in_specs=[anywhere, anywhere, anywhere, anywhere],
+        out_specs=vmem,
         scratch_shapes=[
+            pltpu.SMEM(span_order.shape, jnp.int32),
             pltpu.VMEM((n, 2, local_rows, head_size), jnp.bfloat16),
             pltpu.VMEM((local_rows, width), jnp.bfloat16),
             pltpu.VMEM((2, head_size, rows), jnp.bfloat16),
-            pltpu.VMEM((2, tall, rows), jnp.float32),
             pltpu.VMEM((2, 8, rows), jnp.float32),
             pltpu.VMEM((16, span, 2 * span), jnp.float32),
             pltpu.VMEM((4, 4 * span, 2 * span), jnp.bfloat16),
             pltpu.VMEM((3 * tall, 4 * span), jnp.bfloat16),
-            pltpu.SemaphoreType.DMA((3,)),
-            pltpu.SemaphoreType.DMA((n, 2, 4)),
-            pltpu.SemaphoreType.DMA((n, 2)),
+            pltpu.SemaphoreType.DMA((4,)),
+            pltpu.SemaphoreType.DMA((4,)),
+            pltpu.SemaphoreType.DMA((n // 4, 2, PIECES)),
+            pltpu.SemaphoreType.DMA((n // 4, 2, PIECES)),
+            pltpu.SemaphoreType.DMA((n // 4, 2)),
         ],
-        compiler_params=pltpu.CompilerParams(collective_id=0, has_side_effects=True),
+        compiler_params=pltpu.CompilerParams(
+            collective_id=0, has_side_effects=True, vmem_limit_bytes=GRANT
+        ),
         name="fused",
-    )(span_order, queries, keys, values)
+    )(*(pltpu.with_memory_space_constraint(x, pltpu.HBM) for x in (span_order, queries, keys, values)))
+    return pl.pallas_call(
+        functools.partial(share_kernel, heads, span),
+        out_shape=jax.ShapeDtypeStruct((local_rows, width), jnp.bfloat16),
+        in_specs=[pl.BlockSpec(memory_space=pltpu.SMEM), vmem],
+        out_specs=vmem,
+        compiler_params=pltpu.CompilerParams(vmem_limit_bytes=GRANT),
+        name="share",
+    )(span_order, acc)
 
 
 def body(n, queries, keys, values, span_order):

time: 29.3 us -> 25.2 us (0.86)
  Pallas kernels: 27.3 us -> 25 us
  local copies, waits for them, and re-layouts: 1.87 us -> 0.01 us
    pallas_call x1, Pallas kernels: 27.3 us -> 23.5 us  [fused(): pl.pallas_call(functools.partial(fused_kernel, n, heads, span), out_shape...]
    unnamed x1 -> x2, local copies, waits for them, and re-layouts: 1.87 us -> 0.01 us
    pallas_call x0 -> x1, Pallas kernels: none -> 1.55 us  [fused(): pl.pallas_call(functools.partial(share_kernel, heads, span), out_shape=ja...]
where the time goes in v2:
time: 25.2 us; the launch traced here: 25 us
  Pallas kernels  25 us (99%)
    pallas_call x1, Pallas kernels, fused(): pl.pallas_call(functools.partial(fused_kernel, n, heads, span), out_shape...  23.5 us
    pallas_call x1, Pallas kernels, fused(): pl.pallas_call(functools.partial(share_kernel, heads, span), out_shape=ja...  1.55 us

profile of v2, /device:TPU:0, one launch (start us, length us, event | category | flops | bytes accessed | tf_op | source)
XLA Modules:
  0.0 25.0 jit_solution(7047985279707816132)
XLA Ops:
  0.0 0.0 copy-start
  0.0 23.5 %fused.1.acc = f32[2,144,1024]{2,1,0:T(8,128)S(1)} custom-call(s32[32]{0:T(128)} %order_ref.1, bf16[256,1024]{1,0:T(8,128)(2,1)} %q_hbm.1, bf16[256,128]{1,0:T(8,128)(2,1)} %k_hbm.1, bf16[256,128]{1,0:T(8,128)(2,1)} %v_hbm.1), custom_call_target="tpu_custom_call" | custom-call | tf_op jit(solution)/shard_map/fused/pallas_call | solution.py:624
  23.5 0.0 copy-done
  23.5 1.5 %share.1 = bf16[256,1024]{1,0:T(8,128)(2,1)} custom-call(s32[32]{0:T(128)S(1)} %copy-done, f32[2,144,1024]{2,1,0:T(8,128)S(1)} %fused.1.acc), custom_call_target="tpu_custom_call" | custom-call | tf_op jit(solution)/shard_map/share/pallas_call | solution.py:649
Async XLA Ops:
  0.0 23.5 %copy-start = (s32[32]{0:T(128)S(1)}, s32[32]{0:T(128)}, u32[]{:S(2)}) copy-start(s32[32]{0:T(128)} %order_ref.1) | copy-start | bytes 388

commit v3 on v2

--- a/solution.py
+++ b/solution.py
@@ -12,7 +12,7 @@
 NEG = -1e30
 FUSED_MOST = 32
 PIECES = 2
-RELIEF = True
+EARLY = ((0, 0), (0, 1), (1, 0))
 GRANT = 24 << 20
 
 
@@ -256,8 +256,8 @@
 
 
 def fused_kernel(
-    n, heads, span, order_hbm, q_hbm, k_hbm, v_hbm, acc,
-    order_ref, buf, q_in, qt, top, raw, part, wide_v, load_sem, send_sem, line_sem, side_sem, twin_sem,
+    n, heads, span, order_hbm, q_hbm, k_hbm, v_hbm, out_ref,
+    order_ref, buf, q_in, qt, acc, top, raw, part, wide_v, keys_h, keys_x, load_sem, send_sem, line_sem, side_sem, twin_sem,
 ):
     lanes = 4
     zs = n // lanes
@@ -333,8 +333,11 @@
     at_bottom = z == 0
     at_top = z == zs - 1
 
-    def early(zz, kv):
-        if kv == 0 or zs <= 2 or not RELIEF:
+    def can_be_early(kv, i):
+        return zs > 2 and (kv, i) in EARLY
+
+    def early(zz, kv, i):
+        if not can_be_early(kv, i):
             return jnp.bool_(False)
         return jnp.logical_or(zz == 0, zz == zs - 1)
 
@@ -348,17 +351,17 @@
 
     def sends_line(zz, kv, i, onward, act):
         pl.when(not_top if onward == UP else not_bottom)(lambda: act(copy(zz, y, kv, i, onward)))
-        pl.when(jnp.logical_not(early(zz, kv)))(lambda: act(copy(zz, y, kv, i, SIDE)))
+        pl.when(jnp.logical_not(early(zz, kv, i)))(lambda: act(copy(zz, y, kv, i, SIDE)))
         act(copy(zz, y, kv, i, TWIN))
 
     def sends_side(zz, kv, i, onward, act):
         more = not_top if onward == UP else not_bottom
-        if kv == 1 and zs > 2 and RELIEF:
-            pl.when(jnp.logical_and(early(zz, kv), more))(lambda: act(copy(zz, far_y, kv, i, onward)))
+        if can_be_early(kv, i):
+            pl.when(jnp.logical_and(early(zz, kv, i), more))(lambda: act(copy(zz, far_y, kv, i, onward)))
         act(copy(zz, far_y, kv, i, TWIN))
 
     def sends_near(kv, i, act):
-        if kv == 1 and zs > 2 and RELIEF:
+        if can_be_early(kv, i):
             pl.when(at_bottom)(lambda: act(copy(z, far_y, kv, i, UP)))
             pl.when(at_top)(lambda: act(copy(z, far_y, kv, i, DOWN)))
         act(copy(z, far_y, kv, i, TWIN))
@@ -401,27 +404,26 @@
         pltpu.make_async_copy(where, where, twin_sem.at[zz, int(yy is not y)]).wait()
 
     def all_sent():
-        def taken(arrays, route):
-            blocks = arrays // 2
-            where = buf.at[pl.ds(0, blocks)] if blocks else buf.at[0, 0]
+        def taken(pieces, route):
+            if pieces % (2 * PIECES) == 0:
+                where = buf.at[pl.ds(0, pieces // (2 * PIECES))]
+            else:
+                where = buf.at[0, pl.ds(0, 2), pl.ds(0, pieces * piece // 2)]
             pltpu.make_async_copy(where, where, send_sem.at[route]).wait()
 
-        taken(4 * zs, TWIN)
-        if not RELIEF or zs <= 2:
-            taken(2 * zs, SIDE)
-            for zz in range(zs):
-                pl.when(jnp.logical_and(not_top, zz <= z))(lambda: taken(2, UP))
-                pl.when(jnp.logical_and(not_bottom, zz >= z))(lambda: taken(2, DOWN))
-        else:
-            taken(2, SIDE)
-            for zz in range(zs):
-                pl.when(zz != z)(lambda: taken(1, SIDE))
-                if 0 < zz < zs - 1:
-                    pl.when(zz != z)(lambda: taken(1, SIDE))
-                pl.when(jnp.logical_and(not_top, zz <= z))(lambda: taken(2, UP))
-                pl.when(jnp.logical_and(not_bottom, zz >= z))(lambda: taken(2, DOWN))
-            pl.when(not_top)(lambda: taken(1, UP))
-            pl.when(not_bottom)(lambda: taken(1, DOWN))
+        whole = 2 * PIECES
+        few = len(EARLY) if zs > 2 else 0
+        taken(2 * zs * whole, TWIN)
+        taken(whole, SIDE)
+        for zz in range(zs):
+            kept_back = few if zz in (0, zs - 1) else 0
+            if whole > kept_back:
+                pl.when(zz != z)(lambda: taken(whole - kept_back, SIDE))
+            pl.when(jnp.logical_and(not_top, zz <= z))(lambda: taken(whole, UP))
+            pl.when(jnp.logical_and(not_bottom, zz >= z))(lambda: taken(whole, DOWN))
+        if few:
+            pl.when(not_top)(lambda: taken(few, UP))
+            pl.when(not_bottom)(lambda: taken(few, DOWN))
 
     sends_own(begin)
 
@@ -460,111 +462,217 @@
     def spread(m):
         return jnp.broadcast_to(jnp.max(m, axis=0, keepdims=True), (8, tile))
 
-    def weigh(slot, m):
-        score = raw[slot].reshape(span // 8, 8, tile)
-        return jnp.exp2(score - m[None]).reshape(span, tile).astype(jnp.bfloat16)
-
-    def scores(keys, which, t):
-        return (
-            jnp.dot(keys, qt[which, :, lane_tile(t)], preferred_element_type=jnp.float32) * factor
-        )
-
     def halves_of(d, kv, flip):
         a = buf[d, kv, spans[0], :]
         b = buf[d, kv, spans[1], :]
         return jnp.where(flip, b, a), jnp.where(flip, a, b)
 
+    def nth(j):
+        return slice(j * span, (j + 1) * span)
+
+    kept = lax.broadcasted_iota(jnp.int32, (span, tile), 0) <= lax.rem(
+        lax.broadcasted_iota(jnp.int32, (span, tile), 1), span
+    )
     ones = jnp.ones((EXTRA, span), jnp.bfloat16)
     wide_v[head_size:tall, :] = jnp.ones_like(wide_v[head_size:tall, :])
 
-    def own():
-        k_low, k_high = halves_of(me, 0, swapped)
-        v_low, v_high = halves_of(me, 1, swapped)
-        wide_v[:head_size, :span] = v_low.T
-        wide_v[:head_size, span : 2 * span] = v_high.T
-        kept = lax.broadcasted_iota(jnp.int32, (span, tile), 0) <= lax.rem(
-            lax.broadcasted_iota(jnp.int32, (span, tile), 1), span
-        )
-        for t in range(tiles):
-            lt = lane_tile(t)
-            s0 = scores(k_low, HIGH, t)
-            s1 = jnp.where(kept, scores(k_high, HIGH, t), NEG)
-            s2 = jnp.where(kept, scores(k_low, LOW, t), NEG)
-            raw[0], raw[1], raw[2] = s0, s1, s2
-            m_high = spread(jnp.maximum(peak(s0), peak(s1)))
-            m_low = spread(peak(s2))
-            top[HIGH, :, lt] = m_high
-            top[LOW, :, lt] = m_low
-            part[0, :span, :] = weigh(0, m_high)
-            part[0, span : 2 * span, :] = weigh(1, m_high)
-            part[1, :span, :] = weigh(2, m_low)
-            acc[HIGH, :, lt] = jnp.dot(
-                wide_v[:tall, : 2 * span], part[0, : 2 * span, :], preferred_element_type=jnp.float32
-            )
-            acc[LOW, :, lt] = jnp.dot(
-                wide_v[:tall, :span], part[1, :span, :], preferred_element_type=jnp.float32
-            )
-
-    def group(blocks, between=()):
-        g = len(blocks)
-        depth = g * span
-        info = []
-        for j, d in enumerate(blocks):
+    def group(blocks, first=False, final=False):
+        high_masks, x_units = [], []
+
+        def add_high(keys, masked):
+            keys_h[nth(len(high_masks)), :] = keys
+            high_masks.append(masked)
+
+        def add_x(keys, is_low, masked):
+            keys_x[nth(len(x_units)), :] = keys
+            x_units.append((is_low, masked))
+
+        def values_high(j, values):
+            wide_v[:head_size, nth(j)] = values.T
+
+        def values_x(j, values):
+            is_low = x_units[j][0]
+            at_j = nth(j)
+            turned = values.T
+            nil, none = jnp.zeros_like(turned), jnp.zeros_like(ones)
+            if is_low is True:
+                parts = (turned, ones, nil, none)
+            else:
+                parts = (
+                    jnp.where(is_low, turned, nil),
+                    jnp.where(is_low, ones, none),
+                    jnp.where(is_low, nil, turned),
+                    jnp.where(is_low, none, ones),
+                )
+            wide_v[tall : tall + head_size, at_j] = parts[0]
+            wide_v[tall + head_size : 2 * tall, at_j] = parts[1]
+            wide_v[2 * tall : 2 * tall + head_size, at_j] = parts[2]
+            wide_v[2 * tall + head_size :, at_j] = parts[3]
+
+        if first:
+            k_low, k_high = halves_of(me, 0, swapped)
+            add_high(k_low, False)
+            add_high(k_high, True)
+            add_x(k_low, True, True)
+        for d in blocks:
             q, flip = pair_of(d)
             is_low = q < p
             k_low, k_high = halves_of(d, 0, flip)
-            v_low, v_high = halves_of(d, 1, flip)
-            at_j = slice(j * span, (j + 1) * span)
-            wide_v[:head_size, at_j] = v_low.T
-            v_x = jnp.where(is_low, v_low, v_high).T
-            nil = jnp.zeros_like(v_x)
-            wide_v[tall : tall + head_size, at_j] = jnp.where(is_low, v_x, nil)
-            wide_v[tall + head_size : 2 * tall, at_j] = jnp.where(is_low, ones, jnp.zeros_like(ones))
-            wide_v[2 * tall : 2 * tall + head_size, at_j] = jnp.where(is_low, nil, v_x)
-            wide_v[2 * tall + head_size :, at_j] = jnp.where(is_low, jnp.zeros_like(ones), ones)
-            info.append((is_low, k_low, jnp.where(is_low, k_low, k_high)))
+            add_high(k_low, False)
+            add_x(jnp.where(is_low, k_low, k_high), is_low, False)
+
+        def turn_values():
+            high, x = 0, 0
+            if first:
+                v_low, v_high = halves_of(me, 1, swapped)
+                values_high(0, v_low)
+                values_high(1, v_high)
+                values_x(0, v_low)
+                high, x = 2, 1
+            for j, d in enumerate(blocks):
+                v_low, v_high = halves_of(d, 1, pair_of(d)[1])
+                values_high(high + j, v_low)
+                values_x(x + j, jnp.where(x_units[x + j][0], v_low, v_high))
+
+        turn_values()
+        n_high, n_x = len(high_masks), len(x_units)
+        units = n_high + n_x
+
+        def base(t):
+            return t * units if final else (t % 2) * 8
+
+        def weights_at(t, of_x):
+            if final:
+                return t, of_x * n_high * span
+            return (t % 2) * 2 + of_x, 0
+
+        peaks = {}
+
+        def start_tile(t):
+            lt = lane_tile(t)
+            if first:
+                low = high = jnp.full((8, tile), NEG, jnp.float32)
+            else:
+                high, low = top[HIGH, :, lt], top[LOW, :, lt]
+            peaks[t] = [high, low, high, low]
+
+        def score_steps(t):
+            lt = lane_tile(t)
+
+            def of_high(lo, hi):
+                found = jnp.dot(
+                    keys_h[lo * span : hi * span, :], qt[HIGH, :, lt], preferred_element_type=jnp.float32
+                )
+                for u in range(lo, hi):
+                    s = found[nth(u - lo)]
+                    if high_masks[u]:
+                        s = jnp.where(kept, s, NEG)
+                    raw[base(t) + u] = s
+                    peaks[t][2] = jnp.maximum(peaks[t][2], peak(s))
+
+            def of_x(u):
+                is_low, masked = x_units[u]
+                which = LOW if is_low is True else 1 - is_low.astype(jnp.int32)
+                s = jnp.dot(keys_x[nth(u), :], qt[which, :, lt], preferred_element_type=jnp.float32)
+                if masked:
+                    s = jnp.where(kept, s, NEG)
+                raw[base(t) + n_high + u] = s
+                m = peak(s)
+                if is_low is True:
+                    peaks[t][3] = jnp.maximum(peaks[t][3], m)
+                else:
+                    peaks[t][3] = jnp.where(is_low, jnp.maximum(peaks[t][3], m), peaks[t][3])
+                    peaks[t][2] = jnp.where(is_low, peaks[t][2], jnp.maximum(peaks[t][2], m))
+
+            steps = [
+                functools.partial(of_high, lo, min(lo + 2, n_high)) for lo in range(0, n_high, 2)
+            ]
+            return steps + [functools.partial(of_x, u) for u in range(n_x)]
+
+        def end_tile(t):
+            lt = lane_tile(t)
+            peaks[t][2:] = [spread(peaks[t][2]), spread(peaks[t][3])]
+            top[HIGH, :, lt] = peaks[t][2]
+            top[LOW, :, lt] = peaks[t][3]
+
+        def weigh_steps(t):
+            def weigh(u):
+                if u < n_high:
+                    m, row = peaks[t][2], u
+                else:
+                    is_low = x_units[u - n_high][0]
+                    m = peaks[t][3] if is_low is True else jnp.where(is_low, peaks[t][3], peaks[t][2])
+                    row = u - n_high
+                dest, start = weights_at(t, int(u >= n_high))
+                s = raw[base(t) + u].reshape(span // 8, 8, tile)
+                w = jnp.exp2((s - m[None]) * factor)
+                part[dest, start + row * span : start + (row + 1) * span, :] = w.reshape(span, tile).astype(jnp.bfloat16)
+
+            return [functools.partial(weigh, u) for u in range(units)]
+
+        def gather_values(t):
+            lt = lane_tile(t)
+            a, a0 = weights_at(t, 0)
+            b, b0 = weights_at(t, 1)
+            more = jnp.dot(
+                wide_v[:tall, : n_high * span],
+                part[a, a0 : a0 + n_high * span, :],
+                preferred_element_type=jnp.float32,
+            )
+            both_rows = jnp.dot(
+                wide_v[tall:, : n_x * span],
+                part[b, b0 : b0 + n_x * span, :],
+                preferred_element_type=jnp.float32,
+            )
+            if first:
+                acc[HIGH, :, lt] = more + both_rows[tall:]
+                acc[LOW, :, lt] = both_rows[:tall]
+                return
+
+            def scaled(which, old, new):
+                shrink = jnp.exp2((old - new) * factor)
+                return (acc[which, :, lt].reshape(tall // 8, 8, tile) * shrink[None]).reshape(tall, tile)
+
+            high = scaled(HIGH, peaks[t][0], peaks[t][2]) + (more + both_rows[tall:])
+            low = scaled(LOW, peaks[t][1], peaks[t][3]) + both_rows[:tall]
+            if not final:
+                acc[HIGH, :, lt] = high
+                acc[LOW, :, lt] = low
+                return
+            rows_of = []
+            for whole in (low, high):
+                total = jnp.float32(1.0) / whole[head_size : head_size + 8]
+                share = whole[:head_size].reshape(head_size // 8, 8, tile) * total[None]
+                rows_of.append(share.reshape(head_size, tile).astype(jnp.bfloat16))
+            for k in range(tile // span):
+                low_rows, high_rows = (one[:, nth(k)].T for one in rows_of)
+                cols = slice((t * (tile // span) + k) * head_size, (t * (tile // span) + k + 1) * head_size)
+                out_ref[spans[0], cols] = jnp.where(swapped, high_rows, low_rows)
+                out_ref[spans[1], cols] = jnp.where(swapped, low_rows, high_rows)
+
+        start_tile(0)
+        for step in score_steps(0):
+            step()
+        end_tile(0)
         for t in range(tiles):
-            lt = lane_tile(t)
-            old_high = top[HIGH, :, lt]
-            old_low = top[LOW, :, lt]
-            high, low = old_high, old_low
-            base = (t % 2) * 8
-            for j, (is_low, k_low, k_x) in enumerate(info):
-                s = scores(k_low, HIGH, t)
-                raw[base + 2 * j] = s
-                high = jnp.maximum(high, peak(s))
-                s = scores(k_x, 1 - is_low.astype(jnp.int32), t)
-                raw[base + 2 * j + 1] = s
-                m = peak(s)
-                low = jnp.where(is_low, jnp.maximum(low, m), low)
-                high = jnp.where(is_low, high, jnp.maximum(high, m))
-            high = spread(high)
-            low = spread(low)
-            top[HIGH, :, lt] = high
-            top[LOW, :, lt] = low
-            pb = (t % 2) * 2
-            for j, (is_low, _, _) in enumerate(info):
-                at_j = slice(j * span, (j + 1) * span)
-                part[pb, at_j, :] = weigh(base + 2 * j, high)
-                part[pb + 1, at_j, :] = weigh(base + 2 * j + 1, jnp.where(is_low, low, high))
-            more = jnp.dot(
-                wide_v[:tall, :depth], part[pb, :depth, :], preferred_element_type=jnp.float32
-            )
-            mixed = jnp.dot(
-                wide_v[tall:, :depth], part[pb + 1, :depth, :], preferred_element_type=jnp.float32
-            )
-
-            def scaled(which, old, new):
-                return (
-                    acc[which, :, lt].reshape(tall // 8, 8, tile) * jnp.exp2(old - new)[None]
-                ).reshape(tall, tile)
-
-            acc[HIGH, :, lt] = scaled(HIGH, old_high, high) + (more + mixed[tall:])
-            acc[LOW, :, lt] = scaled(LOW, old_low, low) + mixed[:tall]
-            if t < len(between):
-                between[t]()
-
-    own()
+            ahead = []
+            if t + 1 < tiles:
+                start_tile(t + 1)
+                ahead = score_steps(t + 1)
+            now = weigh_steps(t)
+            for k in range(max(len(ahead), len(now))):
+                if k < len(ahead):
+                    ahead[k]()
+                if k < len(now):
+                    now[k]()
+            if not final:
+                gather_values(t)
+            if t + 1 < tiles:
+                end_tile(t + 1)
+        if final:
+            for t in range(tiles):
+                gather_values(t)
+
     def run(todo):
         for one in todo:
             one()
@@ -572,44 +680,21 @@
     def mixed(a, b):
         return [one for pair in zip(a, b) for one in pair]
 
+    def pair(r, yy):
+        from_twin(plane(r), yy)
+        return [at(plane(r), yy, c), at(plane(r), yy, 1 - c)]
+
+    from_twin(z, y)
+    group([twin], first=True)
     run(mixed(events(line_event, 1), events(side_event, 0)))
-    from_twin(z, y)
-    from_twin(z, far_y)
-    group([twin, side, at(z, 1 - y, 1 - c)])
-    for r in range(1, zs):
-        if r + 1 < zs:
-            run(mixed(events(line_event, r + 1), events(side_event, r)))
+    for r in range(zs - 1):
+        group(pair(r, far_y) + pair(r + 1, y))
+        if r + 2 < zs:
+            run(mixed(events(line_event, r + 2), events(side_event, r + 1)))
         else:
-            run(events(side_event, r))
-        zz = plane(r)
-        if r + 1 == zs:
-            from_twin(zz, y)
-            group([at(zz, y, c), at(zz, y, 1 - c)])
-            from_twin(zz, far_y)
-            group([at(zz, 1 - y, c), at(zz, 1 - y, 1 - c)])
-        else:
-            from_twin(zz, y)
-            from_twin(zz, far_y)
-            group([at(zz, y, c), at(zz, y, 1 - c), at(zz, 1 - y, c), at(zz, 1 - y, 1 - c)])
-
+            run(events(side_event, r + 1))
+    group(pair(zs - 1, far_y), final=True)
     all_sent()
-
-
-def share_kernel(heads, span, order_ref, acc, out_ref):
-    head_size = out_ref.shape[1] // heads
-    spans = (slice(0, span), slice(span, 2 * span))
-    me = lax.axis_index("ctx")
-    swapped = order_ref[2 * me + 1] < order_ref[2 * me]
-    for h in range(heads):
-        cols = slice(h * head_size, (h + 1) * head_size)
-        src = slice(h * span, (h + 1) * span)
-        outs = []
-        for which in (LOW, HIGH):
-            total = acc[which, head_size : head_size + 8, src]
-            share = acc[which, :head_size, src].reshape(head_size // 8, 8, span) / total[None]
-            outs.append(share.reshape(head_size, span).astype(jnp.bfloat16).T)
-        out_ref[spans[0], cols] = jnp.where(swapped, outs[HIGH], outs[LOW])
-        out_ref[spans[1], cols] = jnp.where(swapped, outs[LOW], outs[HIGH])
 
 
 def fused(n, queries, keys, values, span_order):
@@ -621,9 +706,9 @@
     anywhere = pl.BlockSpec(memory_space=pltpu.HBM)
     tall = head_size + EXTRA
     vmem = pl.BlockSpec(memory_space=pltpu.VMEM)
-    acc = pl.pallas_call(
+    return pl.pallas_call(
         functools.partial(fused_kernel, n, heads, span),
-        out_shape=jax.ShapeDtypeStruct((2, tall, rows), jnp.float32),
+        out_shape=jax.ShapeDtypeStruct((local_rows, width), jnp.bfloat16),
         in_specs=[anywhere, anywhere, anywhere, anywhere],
         out_specs=vmem,
         scratch_shapes=[
@@ -631,10 +716,13 @@
             pltpu.VMEM((n, 2, local_rows, head_size), jnp.bfloat16),
             pltpu.VMEM((local_rows, width), jnp.bfloat16),
             pltpu.VMEM((2, head_size, rows), jnp.bfloat16),
+            pltpu.VMEM((2, tall, rows), jnp.float32),
             pltpu.VMEM((2, 8, rows), jnp.float32),
             pltpu.VMEM((16, span, 2 * span), jnp.float32),
             pltpu.VMEM((4, 4 * span, 2 * span), jnp.bfloat16),
             pltpu.VMEM((3 * tall, 4 * span), jnp.bfloat16),
+            pltpu.VMEM((4 * span, head_size), jnp.bfloat16),
+            pltpu.VMEM((4 * span, head_size), jnp.bfloat16),
             pltpu.SemaphoreType.DMA((4,)),
             pltpu.SemaphoreType.DMA((4,)),
             pltpu.SemaphoreType.DMA((n // 4, 2, PIECES)),
@@ -646,14 +734,6 @@
         ),
         name="fused",
     )(*(pltpu.with_memory_space_constraint(x, pltpu.HBM) for x in (span_order, queries, keys, values)))
-    return pl.pallas_call(
-        functools.partial(share_kernel, heads, span),
-        out_shape=jax.ShapeDtypeStruct((local_rows, width), jnp.bfloat16),
-        in_specs=[pl.BlockSpec(memory_space=pltpu.SMEM), vmem],
-        out_specs=vmem,
-        compiler_params=pltpu.CompilerParams(vmem_limit_bytes=GRANT),
-        name="share",
-    )(span_order, acc)
 
 
 def body(n, queries, keys, values, span_order):

time: 25.2 us -> 22.4 us (0.89)
  Pallas kernels: 25 us -> 21.4 us
  local copies, waits for them, and re-layouts: 0.01 us -> 0.8 us
    pallas_call x1, Pallas kernels: 23.5 us -> 21.4 us  [fused(): pl.pallas_call(functools.partial(fused_kernel, n, heads, span), out_shape...]
    pallas_call x1 -> x0, Pallas kernels: 1.55 us -> none  [fused(): pl.pallas_call(functools.partial(share_kernel, heads, span), out_shape=ja...]
    unnamed x2 -> x1, local copies, waits for them, and re-layouts: 0.01 us -> 0.8 us
where the time goes in v3:
time: 22.4 us; the launch traced here: 22.2 us
  Pallas kernels  21.4 us (96%)
  local copies, waits for them, and re-layouts  0.8 us (4%)
    pallas_call x1, Pallas kernels, fused(): pl.pallas_call(functools.partial(fused_kernel, n, heads, span), out_shape...  21.4 us
    unnamed x1, local copies, waits for them, and re-layouts  0.8 us

profile of v3, /device:TPU:0, one launch (start us, length us, event | category | flops | bytes accessed | tf_op | source)
XLA Modules:
  0.0 22.2 jit_solution(14490164284276207940)
XLA Ops:
  0.0 21.4 %fused.1 = bf16[256,1024]{1,0:T(8,128)(2,1)S(1)} custom-call(s32[32]{0:T(128)} %order_hbm.1, bf16[256,1024]{1,0:T(8,128)(2,1)} %q_hbm.1, bf16[256,128]{1,0:T(8,128)(2,1)} %k_hbm.1, bf16[256,128]{1,0:T(8,128)(2,1)} %v_hbm.1), custom_call_target="tpu_custom_call" | custom-call | tf_op jit(solution)/shard_map/fused/pallas_call | solution.py:709
  21.4 0.8 %copy.6 = bf16[256,1024]{1,0:T(8,128)(2,1)} copy(bf16[256,1024]{1,0:T(8,128)(2,1)S(1)} %fused.1) | data formatting | bytes 1048576
